TPU v7x, 512 devices: a whole 4x4x16 slice. The times are simulated.
512 devices in a mesh: cfg: 2 (over y_hi), win: 256 (over x, z, y_lo, core).
Axes of the slice: x: 4, y: 4 (y_hi: 2, y_lo: 2; y = y_hi * 2 + y_lo), z: 16, core: 2. Of those that a mesh axis runs over, the one named last changes fastest.
Arguments:
- latent: float32 [8192, 4, 32], P('win'), may hold values from -6 to 6
- text_kv: bfloat16 [2, 2, 120, 576], P(None, None, None, 'cfg'), may hold values from -200 to 200, as said below
- modulation: float32 [20, 4, 1152], replicated, may hold values from -3 to 3
- qkv_weight: bfloat16 [1152, 3, 576], P(None, None, 'cfg'), may hold values from -0.1875 to 0.1875
- out_weight: bfloat16 [576, 1152], P('cfg'), may hold values from -0.25 to 0.25
- patch_weight: bfloat16 [16, 1152], replicated, may hold values from -1.5 to 1.5
- final_weight: bfloat16 [1152, 16], replicated, may hold values from -0.1875 to 0.1875
- offsets: int32 [256], P('win'), may hold values from 1 to 16
- blend_weights: int32 [256], P('win'), may hold values from 1 to 4
- step_index: int32 [1], replicated, may hold values from 0 to 999
Outputs:
- previous: float32 [8192, 4, 32], P('win', None, 'cfg')
- noise: float32 [8192, 4, 32], P('win', None, 'cfg')
Inputs may be any that keep to these rules, and one draw needn't show every extreme that they name: Window i starts offsets[i] columns before column i * 32. `text_kv`: keys and values of caption tokens.
All inputs are finite; a program needn't handle non-finite values.
Results may differ from a plain program's by a relative error of at most 0.024.
Values may be sent and summed in bfloat16 or wider, within the bound.
A program may use at most 64 MiB of HBM per device.

v0:
```python
import math

import jax
import jax.numpy as jnp
from jax import lax
from jax.sharding import PartitionSpec as P

HEAD_DIM = 72
STEPS = 20


guidance_scale = 4.5
plan_length = 1000
norm_eps = 1e-06


def from_behind(array, axis, by):
    size = lax.axis_size(axis)
    return lax.ppermute(array, axis, [(i, (i + by) % size) for i in range(size)])


def split_up(array, dim, size):
    dims = array.shape
    tiles = array.reshape(*dims[:dim], size, dims[dim] // size, *dims[dim + 1 :])
    return jnp.moveaxis(tiles, dim, 0)


def summed_on_arrival(array, axis, dim):
    tiles = split_up(array, dim, lax.axis_size(axis))
    arrived = lax.all_to_all(tiles, axis, split_axis=0, concat_axis=0, tiled=True)
    return arrived.astype(jnp.float32).sum(axis=0)


def from_partner(value, axis, stride):
    mask = 2**stride
    pairs = [(source, source ^ mask) for source in range(lax.axis_size(axis))]
    return lax.ppermute(value, axis, pairs)


def layer_norm(values):
    average = jnp.mean(values, axis=-1, keepdims=True)
    centered = values - average
    variance = jnp.mean(centered * centered, axis=-1, keepdims=True)
    return centered * lax.rsqrt(variance + norm_eps)


def positions(col_pairs, row_couples, model_width):
    quarter = model_width // 4
    frequency = jnp.exp(-math.log(10000.0) * jnp.arange(quarter, dtype=jnp.float32) / quarter)
    col_pos = jnp.arange(col_pairs, dtype=jnp.float32)[:, None] * frequency[None, :]
    row_pos = jnp.arange(row_couples, dtype=jnp.float32)[:, None] * frequency[None, :]
    col_part = jnp.concatenate([jnp.sin(col_pos), jnp.cos(col_pos)], axis=1)
    row_part = jnp.concatenate([jnp.sin(row_pos), jnp.cos(row_pos)], axis=1)
    half_width = model_width // 2
    pos_table = jnp.concatenate(
        [
            jnp.broadcast_to(row_part[None, :, :], (col_pairs, row_couples, half_width)),
            jnp.broadcast_to(col_part[:, None, :], (col_pairs, row_couples, half_width)),
        ],
        axis=2,
    )
    return pos_table.reshape(col_pairs * row_couples, model_width)


def plan(moment):
    train_grid = jnp.arange(plan_length, dtype=jnp.int32)
    beta_values = 0.0001 + (0.02 - 0.0001) * train_grid.astype(jnp.float32) / (plan_length - 1)
    alpha_bar = jnp.exp(jnp.cumsum(jnp.log(1.0 - beta_values)))
    stride = plan_length // STEPS
    earlier = moment - stride
    alpha_now = jnp.sum(jnp.where(train_grid == moment, alpha_bar, 0.0))
    alpha_before = jnp.sum(jnp.where(train_grid == earlier, alpha_bar, 0.0)) + jnp.where(
        earlier < 0, 1.0, 0.0
    )
    return (alpha_now, alpha_before)


def attend_branches(projected, text_pair, attn_width):
    token_count = projected.shape[0]
    head_count = attn_width // HEAD_DIM
    branches = text_pair.shape[0]
    queries = (
        projected[:, :attn_width].reshape(token_count, head_count, HEAD_DIM).transpose(1, 0, 2)
    )
    keys_own = (
        projected[:, attn_width : 2 * attn_width]
        .reshape(token_count, head_count, HEAD_DIM)
        .transpose(1, 0, 2)
    )
    values_own = (
        projected[:, 2 * attn_width :].reshape(token_count, head_count, HEAD_DIM).transpose(1, 0, 2)
    )
    text_keys = text_pair[:, 0].reshape(branches, -1, head_count, HEAD_DIM).transpose(2, 0, 1, 3)
    text_values = text_pair[:, 1].reshape(branches, -1, head_count, HEAD_DIM).transpose(2, 0, 1, 3)
    factor = 1.0 / math.sqrt(HEAD_DIM)

    def one_head(head_parts):
        query_tile, key_block, value_tile, caption_key_tile, caption_value_tile = head_parts
        own_scores = (
            jnp.einsum("qd,kd->qk", query_tile, key_block, preferred_element_type=jnp.float32)
            * factor
        )
        text_scores = (
            jnp.einsum(
                "cr,eor->eco", query_tile, caption_key_tile, preferred_element_type=jnp.float32
            )
            * factor
        )
        highest = jnp.maximum(jnp.max(own_scores, axis=-1)[None, :], jnp.max(text_scores, axis=-1))
        own_exp = jnp.exp(own_scores[None, :, :] - highest[:, :, None])
        text_exp = jnp.exp(text_scores - highest[:, :, None])
        totals = jnp.sum(own_exp, axis=-1) + jnp.sum(text_exp, axis=-1)
        self_softmax_weights = (own_exp / totals[:, :, None]).astype(jnp.bfloat16)
        caption_softmax_weights = (text_exp / totals[:, :, None]).astype(jnp.bfloat16)
        return jnp.einsum(
            "roz,zt->rot", self_softmax_weights, value_tile, preferred_element_type=jnp.float32
        ) + jnp.einsum(
            "mzc,mce->mze",
            caption_softmax_weights,
            caption_value_tile,
            preferred_element_type=jnp.float32,
        )

    attended = lax.map(one_head, (queries, keys_own, values_own, text_keys, text_values))
    return (
        attended.transpose(1, 2, 0, 3)
        .reshape(branches, token_count, attn_width)
        .astype(jnp.bfloat16)
    )


def on_device(
    latent,
    text_kv,
    modulation,
    qkv_weight,
    out_weight,
    patch_weight,
    final_weight,
    offsets,
    blend_weights,
    step_index,
):
    slab_cols = latent.shape[0]
    model_width = patch_weight.shape[1]
    half_attn = out_weight.shape[0]
    branch = lax.axis_index("cfg")
    lead_cols = slab_cols // 2
    tail_cols = from_behind(latent[slab_cols - lead_cols :], "win", 1)
    following = from_behind(latent, "win", -1)
    extended = jnp.concatenate([tail_cols, latent, following], axis=0)
    start_at = lead_cols - offsets[0]
    window = lax.dynamic_slice_in_dim(extended, start_at, 2 * slab_cols, 0)
    moment = step_index[0]
    selected = jnp.arange(STEPS, dtype=jnp.int32) == moment * STEPS // plan_length
    modulate = jnp.sum(jnp.where(selected[:, None, None], modulation, 0.0), axis=0)
    col_count, channels, row_count = window.shape
    col_pairs = col_count // 2
    row_couples = row_count // 2
    patches = window.reshape(col_pairs, 2, channels, row_couples, 2).transpose(0, 3, 1, 2, 4)
    patches = patches.reshape(col_pairs * row_couples, 4 * channels).astype(jnp.bfloat16)
    embedded = jnp.dot(patches, patch_weight, preferred_element_type=jnp.float32) + positions(
        col_pairs, row_couples, model_width
    )
    normed = (layer_norm(embedded) * (1.0 + modulate[1]) + modulate[0]).astype(jnp.bfloat16)
    w_qkv = qkv_weight.reshape(model_width, 3 * half_attn)
    projected = jnp.dot(normed, w_qkv, preferred_element_type=jnp.float32).astype(jnp.bfloat16)
    attended = attend_branches(projected, text_kv, half_attn)
    mixed_sum = summed_on_arrival(
        jnp.einsum("btk,kd->btd", attended, out_weight, preferred_element_type=jnp.float32).astype(
            jnp.bfloat16
        ),
        "cfg",
        0,
    )[0]
    residual = embedded + modulate[2] * mixed_sum
    final_norm = (layer_norm(residual) * (1.0 + modulate[3])).astype(jnp.bfloat16)
    noise_tokens = jnp.dot(final_norm, final_weight, preferred_element_type=jnp.float32)
    unpacked = noise_tokens.reshape(col_pairs, row_couples, 2, channels, 2).transpose(0, 2, 3, 1, 4)
    predicted = unpacked.reshape(col_count, channels, row_count)
    half_rows = row_count // 2
    own_first = branch * half_rows
    other_first = (1 - branch) * half_rows
    kept = lax.dynamic_slice_in_dim(predicted, own_first, half_rows, 2)
    handed = lax.dynamic_slice_in_dim(predicted, other_first, half_rows, 2)
    partner = from_partner(handed, "cfg", 0)
    conditional = jnp.where(branch == 0, kept, partner)
    unconditional = jnp.where(branch == 0, partner, kept)
    guided = unconditional + guidance_scale * (conditional - unconditional)
    weight_value = blend_weights[0].astype(jnp.float32)
    zero_index = jnp.zeros((), jnp.int32)
    extent = extended.shape[0]
    spread = lax.dynamic_update_slice(
        jnp.zeros((extent,) + guided.shape[1:], jnp.float32),
        weight_value * guided,
        (start_at, zero_index, zero_index),
    )
    coverage = lax.dynamic_update_slice(
        jnp.zeros((extent,), jnp.float32),
        jnp.full((2 * slab_cols,), weight_value, jnp.float32),
        (start_at,),
    )
    from_left = from_behind(
        (spread[lead_cols + slab_cols :], coverage[lead_cols + slab_cols :]), "win", 1
    )
    from_right = from_behind((spread[:lead_cols], coverage[:lead_cols]), "win", -1)
    numerator = spread[lead_cols : lead_cols + slab_cols] + from_left[0]
    numerator = numerator.at[slab_cols - lead_cols :].add(from_right[0])
    denominator = coverage[lead_cols : lead_cols + slab_cols] + from_left[1]
    denominator = denominator.at[slab_cols - lead_cols :].add(from_right[1])
    blended = numerator / denominator[:, None, None]
    latent_rows = lax.dynamic_slice_in_dim(latent, own_first, half_rows, 2)
    alpha_now, alpha_before = plan(moment)
    previous = (
        jnp.sqrt(alpha_before)
        * (latent_rows - jnp.sqrt(1.0 - alpha_now) * blended)
        / jnp.sqrt(alpha_now)
        + jnp.sqrt(1.0 - alpha_before) * blended
    )
    return (previous, blended)


def solution(mesh):
    in_specs = (
        P("win", None, None),
        P(None, None, None, "cfg"),
        P(),
        P(None, None, "cfg"),
        P("cfg", None),
        P(),
        P(),
        P("win"),
        P("win"),
        P(),
    )
    out_specs = (P("win", None, "cfg"), P("win", None, "cfg"))
    return jax.shard_map(
        on_device, mesh=mesh, in_specs=in_specs, out_specs=out_specs, check_vma=False
    )
```

profile of v0, /device:TPU:16, one launch (start us, length us, event | category | flops | bytes accessed | tf_op | source)
XLA Modules:
  0.0 129.7 jit_solution(9366662816148679159)
XLA Ops:
  0.6 1.1 copy.49
  1.8 1.9 %collective-permute-start = (bf16[16,4,32]{0,2,1:T(8,128)(2,1)S(1)}, bf16[16,4,32]{0,2,1:T(8,128)(2,1)S(1)}, u32[]{:S(2)}, u32[]{:S(2)}) collective-permute-start(bf16[16,4,32]{0,2,1:T(8,128)(2,1)S(1)} %slice.118), channel_id=1, source_target_pairs={{0,1},{1,2},{2,3},{3,4},{4,5},{5,6},{6,7},{7,8},{8,9},{9,10},{10,1... | collective-permute-start | bytes 12296 | tf_op jit(solution)/shard_map/ppermute | solution.py:19
  3.7 13.8 %collective-permute-start.1 = (bf16[32,4,32]{0,2,1:T(8,128)(2,1)S(1)}, bf16[32,4,32]{0,2,1:T(8,128)(2,1)S(1)}, u32[]{:S(2)}, u32[]{:S(2)}) collective-permute-start(bf16[32,4,32]{0,2,1:T(8,128)(2,1)S(1)} %convert.1), channel_id=1, source_target_pairs={{0,255},{1,0},{2,1},{3,2},{4,3},{5,4},{6,5},{7,6},{8,7},{9,8},{10,... | collective-permute-start | bytes 24584 | tf_op jit(solution)/shard_map/ppermute | solution.py:19
  18.5 1.7 %fusion.42 = (bf16[2,1,120,288]{2,3,1,0:T(8,128)(2,1)}, bf16[2,1,120,288]{2,3,1,0:T(8,128)(2,1)}) fusion(bf16[2,2,120,288]{2,3,1,0:T(8,128)(2,1)} %param.17), kind=kLoop, calls=%fused_computation.96 | loop fusion | bytes 552960 | tf_op jit(solution)/shard_map/slice | solution.py:94
  20.6 1.8 %pad_maximum_fusion = f32[32,16,1152]{2,1,0:T(8,128)} fusion(f32[32,16,576]{2,1,0:T(8,128)S(1)} %broadcast_in_dim.41, f32[32,16,576]{2,1,0:T(8,128)S(1)} %broadcast_in_dim.33), kind=kLoop, calls=%fused_computation.36 | loop fusion | flops 589824 | bytes 4718592 | tf_op jit(solution)/shard_map/concatenate | solution.py:55
  23.5 0.9 copy.53
  24.4 1.2 copy.54
  25.8 2.2 %fusion.43 = (f32[512]{0:T(512)S(1)}, f32[512,1152]{1,0:T(8,128)S(1)}) fusion(f32[512,1152]{1,0:T(8,128)} %bitcast.109, bf16[512,16]{0,1:T(8,128)(2,1)S(1)} %convert_element_type.57, bf16[16,1152]{1,0:T(8,128)(2,1)S(1)} %copy-done.6), kind=kOutput, calls=%fused_computation.97 | convolution fusion | flops 20053504 | bytes 4773888 | tf_op jit(solution)/shard_map/dot_general | solution.py:162
  28.0 0.4 multiply_reduce_fusion.1
  28.4 1.5 %convolution_convert_fusion.1 = bf16[512,864]{0,1:T(8,128)(2,1)S(1)} fusion(bf16[1152,864]{0,1:T(8,128)(2,1)S(1)} %bitcast.108, f32[512,1152]{1,0:T(8,128)S(1)} %get-tuple-element.125, f32[1152]{0:T(1024)S(1)} %get-tuple-element.86, f32[1152]{0:T(1024)S(1)} %get-tuple-element.87, f32[512]{0:T(512)S(1)} %add_rsqrt_fusion.1, f32[512]{0:T(512)S(1)} %broadcast_multiply_fusion.1), kind=kOutput, calls=%fused_computation.42 | convolution fusion | flops 1022607360 | bytes 5248000 | tf_op jit(solution)/shard_map/dot_general | solution.py:167
  29.9 0.9 fusion.41
  30.8 1.0 copy.55
  31.8 38.4 %while.12 = (s32[]{:T(128)}, bf16[4,2,512,72]{2,3,0,1:T(8,128)(2,1)}, bf16[4,512,72]{1,2,0:T(8,128)(2,1)}, bf16[4,512,72]{2,1,0:T(8,128)(2,1)}, bf16[4,2,120,72]...) while((s32[]{:T(128)}, ...), condition=%wide.region_12.13_spmd, body=%wide.region_7.0_spmd.sunk | while | flops 152713728 | bytes 12811917 | solution.py:124
  31.8 1.2 fusion.60
  33.1 1.2 fusion.59
  34.3 1.3 %copy.82 = f32[512,512]{1,0:T(8,128)} copy(f32[512,512]{0,1:T(8,128)S(1)} %get-tuple-element.175) | data formatting | bytes 2097152 | tf_op jit(solution)/shard_map/while/body/eval_jaxpr/mul | solution.py:100
  35.6 1.9 %fusion.61 = f32[2,512]{1,0:T(2,128)S(1)} fusion(f32[2,512]{1,0:T(2,128)S(1)} %broadcast_maximum_fusion.2, f32[512,512]{1,0:T(8,128)} %copy.82), kind=kLoop, calls=%fused_computation.2.clone.1 | loop fusion | flops 1047552 | bytes 1056768 | tf_op jit(solution)/shard_map/while/body/eval_jaxpr/reduce_sum | solution.py:112
  37.6 2.0 %fusion.63 = f32[2,512,72]{1,2,0:T(8,128)S(1)} fusion(f32[2,512]{1,0:T(2,128)S(1)} %add.169, f32[2,512]{1,0:T(2,128)S(1)} %broadcast_maximum_fusion.2, f32[512,512]{1,0:T(8,128)} %copy.82, bf16[4,512,72]{1,2,0:T(8,128)(2,1)} %get-tuple-element.198, s32[]{:T(128)} %get-tuple-element.185), kind=kOutput, calls=%fused_computation.9.clone.1 | convolution fusion | flops 77070336 | bytes 1425920 | tf_op jit(solution)/shard_map/while/body/eval_jaxpr/roz,zt->rot/dot_general | solution.py:115
  39.6 1.0 fusion.64
  40.6 0.8 copy-done.9
  41.4 1.2 fusion.60
  42.7 1.2 fusion.59
  43.9 1.3 %copy.82 = f32[512,512]{1,0:T(8,128)} copy(f32[512,512]{0,1:T(8,128)S(1)} %get-tuple-element.175) | data formatting | bytes 2097152 | tf_op jit(solution)/shard_map/while/body/eval_jaxpr/mul | solution.py:100
  45.2 1.9 %fusion.61 = f32[2,512]{1,0:T(2,128)S(1)} fusion(f32[2,512]{1,0:T(2,128)S(1)} %broadcast_maximum_fusion.2, f32[512,512]{1,0:T(8,128)} %copy.82), kind=kLoop, calls=%fused_computation.2.clone.1 | loop fusion | flops 1047552 | bytes 1056768 | tf_op jit(solution)/shard_map/while/body/eval_jaxpr/reduce_sum | solution.py:112
  47.2 2.0 %fusion.63 = f32[2,512,72]{1,2,0:T(8,128)S(1)} fusion(f32[2,512]{1,0:T(2,128)S(1)} %add.169, f32[2,512]{1,0:T(2,128)S(1)} %broadcast_maximum_fusion.2, f32[512,512]{1,0:T(8,128)} %copy.82, bf16[4,512,72]{1,2,0:T(8,128)(2,1)} %get-tuple-element.198, s32[]{:T(128)} %get-tuple-element.185), kind=kOutput, calls=%fused_computation.9.clone.1 | convolution fusion | flops 77070336 | bytes 1425920 | tf_op jit(solution)/shard_map/while/body/eval_jaxpr/roz,zt->rot/dot_general | solution.py:115
  49.2 1.0 fusion.64
  50.2 0.8 copy-done.9
  51.0 1.2 fusion.60
  52.3 1.2 fusion.59
  53.5 1.3 %copy.82 = f32[512,512]{1,0:T(8,128)} copy(f32[512,512]{0,1:T(8,128)S(1)} %get-tuple-element.175) | data formatting | bytes 2097152 | tf_op jit(solution)/shard_map/while/body/eval_jaxpr/mul | solution.py:100
  54.8 1.9 %fusion.61 = f32[2,512]{1,0:T(2,128)S(1)} fusion(f32[2,512]{1,0:T(2,128)S(1)} %broadcast_maximum_fusion.2, f32[512,512]{1,0:T(8,128)} %copy.82), kind=kLoop, calls=%fused_computation.2.clone.1 | loop fusion | flops 1047552 | bytes 1056768 | tf_op jit(solution)/shard_map/while/body/eval_jaxpr/reduce_sum | solution.py:112
  56.8 2.0 %fusion.63 = f32[2,512,72]{1,2,0:T(8,128)S(1)} fusion(f32[2,512]{1,0:T(2,128)S(1)} %add.169, f32[2,512]{1,0:T(2,128)S(1)} %broadcast_maximum_fusion.2, f32[512,512]{1,0:T(8,128)} %copy.82, bf16[4,512,72]{1,2,0:T(8,128)(2,1)} %get-tuple-element.198, s32[]{:T(128)} %get-tuple-element.185), kind=kOutput, calls=%fused_computation.9.clone.1 | convolution fusion | flops 77070336 | bytes 1425920 | tf_op jit(solution)/shard_map/while/body/eval_jaxpr/roz,zt->rot/dot_general | solution.py:115
  58.8 1.0 fusion.64
  59.8 0.8 copy-done.9
  60.6 1.2 fusion.60
  61.9 1.2 fusion.59
  63.1 1.3 %copy.82 = f32[512,512]{1,0:T(8,128)} copy(f32[512,512]{0,1:T(8,128)S(1)} %get-tuple-element.175) | data formatting | bytes 2097152 | tf_op jit(solution)/shard_map/while/body/eval_jaxpr/mul | solution.py:100
  64.4 1.9 %fusion.61 = f32[2,512]{1,0:T(2,128)S(1)} fusion(f32[2,512]{1,0:T(2,128)S(1)} %broadcast_maximum_fusion.2, f32[512,512]{1,0:T(8,128)} %copy.82), kind=kLoop, calls=%fused_computation.2.clone.1 | loop fusion | flops 1047552 | bytes 1056768 | tf_op jit(solution)/shard_map/while/body/eval_jaxpr/reduce_sum | solution.py:112
  66.4 2.0 %fusion.63 = f32[2,512,72]{1,2,0:T(8,128)S(1)} fusion(f32[2,512]{1,0:T(2,128)S(1)} %add.169, f32[2,512]{1,0:T(2,128)S(1)} %broadcast_maximum_fusion.2, f32[512,512]{1,0:T(8,128)} %copy.82, bf16[4,512,72]{1,2,0:T(8,128)(2,1)} %get-tuple-element.198, s32[]{:T(128)} %get-tuple-element.185), kind=kOutput, calls=%fused_computation.9.clone.1 | convolution fusion | flops 77070336 | bytes 1425920 | tf_op jit(solution)/shard_map/while/body/eval_jaxpr/roz,zt->rot/dot_general | solution.py:115
  68.4 1.0 fusion.64
  69.4 0.8 copy-done.9
  70.2 4.2 %fusion.24 = bf16[2,1,512,1152]{3,2,1,0:T(8,128)(2,1)} fusion(bf16[2,512,288]{1,2,0:T(8,128)(2,1)} %bitcast.120, bf16[288,1152]{1,0:T(8,128)(2,1)} %param.20), kind=kOutput, calls=%fused_computation.35 | convolution fusion | flops 680656896 | bytes 3612672 | tf_op jit(solution)/shard_map/btk,kd->btd/dot_general | solution.py:170
  74.4 5.6 %all-to-all-start = ((bf16[2,1,512,1152]{3,2,1,0:T(8,128)(2,1)}), bf16[2,1,512,1152]{3,2,1,0:T(8,128)(2,1)}, u32[]{:S(2)}, u32[]{:S(2)}) async-start(bf16[2,1,512,1152]{3,2,1,0:T(8,128)(2,1)} %fusion.24), calls=%async_computation | async-start | bytes 4718592 | tf_op jit(solution)/shard_map/all_to_all | solution.py:30
  80.7 1.9 %collective-permute-start.5 = (f32[32]{0:T(128)S(1)}, f32[32]{0:T(128)S(1)}, u32[]{:S(2)}, u32[]{:S(2)}) collective-permute-start(f32[32]{0:T(128)S(1)} %slice.114), channel_id=1, source_target_pairs={{0,1},{1,2},{2,3},{3,4},{4,5},{5,6},{6,7},{7,8},{8,9},{9,10},{10,1... | collective-permute-start | bytes 392 | tf_op jit(solution)/shard_map/ppermute | solution.py:19
  82.7 7.9 %collective-permute-start.6 = (f32[16]{0:T(128)S(1)}, f32[16]{0:T(128)S(1)}, u32[]{:S(2)}, u32[]{:S(2)}) collective-permute-start(f32[16]{0:T(128)S(1)} %bitcast.119), channel_id=1, source_target_pairs={{0,255},{1,0},{2,1},{3,2},{4,3},{5,4},{6,5},{7,6},{8,7},{9,8},{10,... | collective-permute-start | bytes 200 | tf_op jit(solution)/shard_map/ppermute | solution.py:19
  91.1 0.7 select_reduce_fusion.1
  94.0 6.2 %all-to-all-done = bf16[2,1,512,1152]{3,2,1,0:T(8,128)(2,1)} async-done(((bf16[2,1,512,1152]{3,2,1,0:T(8,128)(2,1)}), bf16[2,1,512,1152]{3,2,1,0:T(8,128)(2,1)}, u32[]{:S(2)}, u32[]{:S(2)}) %all-to-all-start) | async-done | bytes 2359328 | tf_op jit(solution)/shard_map/all_to_all | solution.py:30
  100.1 2.5 %convert_reduce_fusion = f32[512,1152]{1,0:T(8,128)S(1)} fusion(bf16[2,1,512,1152]{3,2,1,0:T(8,128)(2,1)} %all-to-all-done), kind=kLoop, calls=%fused_computation.32 | loop fusion | flops 1769472 | bytes 4718592 | tf_op jit(solution)/shard_map/reduce_sum | solution.py:31
  102.7 0.3 fusion.38
  103.0 0.4 multiply_reduce_fusion
  103.4 0.4 copy-done.7
  103.8 0.6 fusion.29
  104.5 1.0 copy.60
  105.5 1.1 constant_dynamic-slice_fusion.1
  106.6 1.3 copy.67
  107.9 5.1 %collective-permute-start.2 = (f32[64,4,16]{0,2,1:T(8,128)S(1)}, f32[64,4,16]{0,2,1:T(8,128)S(1)}, u32[]{:S(2)}, u32[]{:S(2)}) collective-permute-start(f32[64,4,16]{0,2,1:T(8,128)S(1)} %copy.67), channel_id=1, source_target_pairs={{0,256},{256,0},{1,257},{257,1},{2,258},{258,2},{3,259},{259,3},{4... | collective-permute-start | bytes 49160 | tf_op jit(solution)/shard_map/ppermute | solution.py:37
  113.1 1.3 copy.68
  114.4 0.8 collective-permute-done.2
  115.2 0.7 dynamic_update_slice.10
  116.0 1.9 %collective-permute-start.3 = (f32[32,4,16]{0,2,1:T(8,128)S(1)}, f32[32,4,16]{0,2,1:T(8,128)S(1)}, u32[]{:S(2)}, u32[]{:S(2)}) collective-permute-start(f32[32,4,16]{0,2,1:T(8,128)S(1)} %slice.127), channel_id=1, source_target_pairs={{0,1},{1,2},{2,3},{3,4},{4,5},{5,6},{6,7},{7,8},{8,9},{9,10},{10,1... | collective-permute-start | bytes 24584 | tf_op jit(solution)/shard_map/ppermute | solution.py:19
  118.1 8.5 %collective-permute-start.4 = (f32[16,4,16]{0,2,1:T(8,128)S(1)}, f32[16,4,16]{0,2,1:T(8,128)S(1)}, u32[]{:S(2)}, u32[]{:S(2)}) collective-permute-start(f32[16,4,16]{0,2,1:T(8,128)S(1)} %bitcast.117), channel_id=1, source_target_pairs={{0,255},{1,0},{2,1},{3,2},{4,3},{5,4},{6,5},{7,6},{8,7},{9,8},{10,... | collective-permute-start | bytes 12296 | tf_op jit(solution)/shard_map/ppermute | solution.py:19
  126.8 1.5 %collective-permute-done.4 = f32[16,4,16]{0,2,1:T(8,128)S(1)} collective-permute-done((f32[16,4,16]{0,2,1:T(8,128)S(1)}, f32[16,4,16]{0,2,1:T(8,128)S(1)}, u32[]{:S(2)}, u32[]{:S(2)}) %collective-permute-start.4) | collective-permute-done | bytes 4128 | tf_op jit(solution)/shard_map/ppermute | solution.py:19
  128.3 0.7 scatter-add.6
  129.0 0.6 multiply_add_fusion.1
  (81 shorter events, 3.1 us)
Async XLA Ops:
  0.6 27.8 %copy-start = (bf16[1152,3,288]{0,2,1:T(8,128)(2,1)S(1)}, bf16[1152,3,288]{0,2,1:T(8,128)(2,1)}, u32[]{:S(2)}) copy-start(bf16[1152,3,288]{0,2,1:T(8,128)(2,1)} %param.19) | copy-start | bytes 5971972
  1.7 21.6 %copy-start.3 = (f32[32,4,32]{0,2,1:T(8,128)}, f32[32,4,32]{0,2,1:T(8,128)S(1)}, u32[]{:S(2)}) copy-start(f32[32,4,32]{0,2,1:T(8,128)S(1)} %copy.49) | copy-start | bytes 49156
  1.8 21.5 %collective-permute-start = (bf16[16,4,32]{0,2,1:T(8,128)(2,1)S(1)}, bf16[16,4,32]{0,2,1:T(8,128)(2,1)S(1)}, u32[]{:S(2)}, u32[]{:S(2)}) collective-permute-start(bf16[16,4,32]{0,2,1:T(8,128)(2,1)S(1)} %slice.118), channel_id=1, source_target_pairs={{0,1},{1,2},{2,3},{3,4},{4,5},{5,6},{6,7},{7,8},{8,9},{9,10},{10,1... | collective-permute-start | bytes 12296 | tf_op jit(solution)/shard_map/ppermute | solution.py:19
  3.7 19.6 %collective-permute-start.1 = (bf16[32,4,32]{0,2,1:T(8,128)(2,1)S(1)}, bf16[32,4,32]{0,2,1:T(8,128)(2,1)S(1)}, u32[]{:S(2)}, u32[]{:S(2)}) collective-permute-start(bf16[32,4,32]{0,2,1:T(8,128)(2,1)S(1)} %convert.1), channel_id=1, source_target_pairs={{0,255},{1,0},{2,1},{3,2},{4,3},{5,4},{6,5},{7,6},{8,7},{9,8},{10,... | collective-permute-start | bytes 24584 | tf_op jit(solution)/shard_map/ppermute | solution.py:19
  20.6 1.8 %copy-start.5 = (f32[20,4,1152]{2,1,0:T(4,128)S(1)}, f32[20,4,1152]{2,1,0:T(4,128)}, u32[]{:S(2)}) copy-start(f32[20,4,1152]{2,1,0:T(4,128)} %param.18) | copy-start | bytes 1105924
  20.6 5.2 %copy-start.6 = (bf16[16,1152]{1,0:T(8,128)(2,1)S(1)}, bf16[16,1152]{1,0:T(8,128)(2,1)}, u32[]{:S(2)}) copy-start(bf16[16,1152]{1,0:T(8,128)(2,1)} %param.21) | copy-start | bytes 110596
  28.0 1.9 %copy-start.1 = (f32[512,1152]{1,0:T(8,128)}, f32[512,1152]{1,0:T(8,128)S(1)}, u32[]{:S(2)}) copy-start(f32[512,1152]{1,0:T(8,128)S(1)} %get-tuple-element.125) | copy-start | bytes 7077892
  37.6 2.0 %copy-start.8 = (bf16[4,2,512,72]{2,3,0,1:T(8,128)(2,1)S(1)}, bf16[4,2,512,72]{2,3,0,1:T(8,128)(2,1)}, u32[]{:S(2)}) copy-start(bf16[4,2,512,72]{2,3,0,1:T(8,128)(2,1)} %get-tuple-element.186) | copy-start | bytes 1769476 | tf_op jit(solution)/shard_map/while
  40.6 0.8 copy-start.9
  47.2 2.0 %copy-start.8 = (bf16[4,2,512,72]{2,3,0,1:T(8,128)(2,1)S(1)}, bf16[4,2,512,72]{2,3,0,1:T(8,128)(2,1)}, u32[]{:S(2)}) copy-start(bf16[4,2,512,72]{2,3,0,1:T(8,128)(2,1)} %get-tuple-element.186) | copy-start | bytes 1769476 | tf_op jit(solution)/shard_map/while
  50.2 0.8 copy-start.9
  56.8 2.0 %copy-start.8 = (bf16[4,2,512,72]{2,3,0,1:T(8,128)(2,1)S(1)}, bf16[4,2,512,72]{2,3,0,1:T(8,128)(2,1)}, u32[]{:S(2)}) copy-start(bf16[4,2,512,72]{2,3,0,1:T(8,128)(2,1)} %get-tuple-element.186) | copy-start | bytes 1769476 | tf_op jit(solution)/shard_map/while
  59.8 0.8 copy-start.9
  66.4 2.0 %copy-start.8 = (bf16[4,2,512,72]{2,3,0,1:T(8,128)(2,1)S(1)}, bf16[4,2,512,72]{2,3,0,1:T(8,128)(2,1)}, u32[]{:S(2)}) copy-start(bf16[4,2,512,72]{2,3,0,1:T(8,128)(2,1)} %get-tuple-element.186) | copy-start | bytes 1769476 | tf_op jit(solution)/shard_map/while
  69.4 0.8 copy-start.9
  74.4 25.7 %all-to-all-start = ((bf16[2,1,512,1152]{3,2,1,0:T(8,128)(2,1)}), bf16[2,1,512,1152]{3,2,1,0:T(8,128)(2,1)}, u32[]{:S(2)}, u32[]{:S(2)}) async-start(bf16[2,1,512,1152]{3,2,1,0:T(8,128)(2,1)} %fusion.24), calls=%async_computation | async-start | bytes 4718592 | tf_op jit(solution)/shard_map/all_to_all | solution.py:30
  80.7 32.3 %collective-permute-start.5 = (f32[32]{0:T(128)S(1)}, f32[32]{0:T(128)S(1)}, u32[]{:S(2)}, u32[]{:S(2)}) collective-permute-start(f32[32]{0:T(128)S(1)} %slice.114), channel_id=1, source_target_pairs={{0,1},{1,2},{2,3},{3,4},{4,5},{5,6},{6,7},{7,8},{8,9},{9,10},{10,1... | collective-permute-start | bytes 392 | tf_op jit(solution)/shard_map/ppermute | solution.py:19
  82.7 35.3 %collective-permute-start.6 = (f32[16]{0:T(128)S(1)}, f32[16]{0:T(128)S(1)}, u32[]{:S(2)}, u32[]{:S(2)}) collective-permute-start(f32[16]{0:T(128)S(1)} %bitcast.119), channel_id=1, source_target_pairs={{0,255},{1,0},{2,1},{3,2},{4,3},{5,4},{6,5},{7,6},{8,7},{9,8},{10,... | collective-permute-start | bytes 200 | tf_op jit(solution)/shard_map/ppermute | solution.py:19
  100.1 2.5 %copy-start.2 = (f32[512,1152]{1,0:T(8,128)S(1)}, f32[512,1152]{1,0:T(8,128)}, u32[]{:S(2)}) copy-start(f32[512,1152]{1,0:T(8,128)} %copy-done.1) | copy-start | bytes 7077892
  103.0 0.8 copy-start.7
  104.5 24.5 %copy-start.4 = (f32[32,4,32]{0,2,1:T(8,128)S(1)}, f32[32,4,32]{0,2,1:T(8,128)}, u32[]{:S(2)}) copy-start(f32[32,4,32]{0,2,1:T(8,128)} %copy-done.3) | copy-start | bytes 49156
  107.9 7.3 %collective-permute-start.2 = (f32[64,4,16]{0,2,1:T(8,128)S(1)}, f32[64,4,16]{0,2,1:T(8,128)S(1)}, u32[]{:S(2)}, u32[]{:S(2)}) collective-permute-start(f32[64,4,16]{0,2,1:T(8,128)S(1)} %copy.67), channel_id=1, source_target_pairs={{0,256},{256,0},{1,257},{257,1},{2,258},{258,2},{3,259},{259,3},{4... | collective-permute-start | bytes 49160 | tf_op jit(solution)/shard_map/ppermute | solution.py:37
  116.0 10.6 %collective-permute-start.3 = (f32[32,4,16]{0,2,1:T(8,128)S(1)}, f32[32,4,16]{0,2,1:T(8,128)S(1)}, u32[]{:S(2)}, u32[]{:S(2)}) collective-permute-start(f32[32,4,16]{0,2,1:T(8,128)S(1)} %slice.127), channel_id=1, source_target_pairs={{0,1},{1,2},{2,3},{3,4},{4,5},{5,6},{6,7},{7,8},{8,9},{9,10},{10,1... | collective-permute-start | bytes 24584 | tf_op jit(solution)/shard_map/ppermute | solution.py:19
  118.1 10.1 %collective-permute-start.4 = (f32[16,4,16]{0,2,1:T(8,128)S(1)}, f32[16,4,16]{0,2,1:T(8,128)S(1)}, u32[]{:S(2)}, u32[]{:S(2)}) collective-permute-start(f32[16,4,16]{0,2,1:T(8,128)S(1)} %bitcast.117), channel_id=1, source_target_pairs={{0,255},{1,0},{2,1},{3,2},{4,3},{5,4},{6,5},{7,6},{8,7},{9,8},{10,... | collective-permute-start | bytes 12296 | tf_op jit(solution)/shard_map/ppermute | solution.py:19
where the time goes:
time: 131 us; the launch traced here: 130 us
  starting transfers between devices  46.6 us (36%)
  matrix products  30 us (23%)
  local copies, waits for them, and re-layouts  22.8 us (17%)
  other arithmetic  16.4 us (13%)
  waiting for transfers between devices  8.44 us (6%)
  between operations  5.15 us (4%)
    ppermute x6, starting transfers between devices, from_behind(): lax.ppermute(array, axis, [(i, (i + by) % size) for i in range(size)])  35.9 us
    reduce_sum x8, other arithmetic, one_head(): totals = jnp.sum(own_exp, axis=-1) + jnp.sum(text_exp, axis=-1)  8.02 us
    dot_general x4, matrix products, one_head(): jnp.einsum('roz,zt->rot', self_softmax_weights, value_tile, preferred_ele...  7.94 us
    all_to_all x1, waiting for transfers between devices, summed_on_arrival(): lax.all_to_all(tiles, axis, split_axis=0, concat_axis=0, tiled=True)  6.16 us
    all_to_all x1, starting transfers between devices, summed_on_arrival(): lax.all_to_all(tiles, axis, split_axis=0, concat_axis=0, tiled=True)  5.55 us
    mul x4, local copies, waits for them, and re-layouts, one_head(): jnp.einsum('qd,kd->qk', query_tile, key_block, preferred_element_type=jnp...  5.23 us
    ppermute x1, starting transfers between devices, from_partner(): return lax.ppermute(value, axis, pairs)  5.13 us
    dot_general x4, matrix products, one_head(): jnp.einsum('qd,kd->qk', query_tile, key_block, preferred_element_type=jnp...  4.9 us
  transfers between devices with their start and end apart: 8, of which 3 were waited for; matrix products, arithmetic and copies ran while one was open for 12% of the time, Pallas kernels for 0%

commit v1 on v0

v1 whole, which is shorter than its diff:
```python
import functools
import math

import jax
import jax.numpy as jnp
import numpy as np
from jax import lax
from jax.experimental import pallas as pl
from jax.experimental.pallas import tpu as pltpu
from jax.sharding import PartitionSpec as P

HEAD_DIM = 72
STEPS = 20

guidance_scale = 4.5
plan_length = 1000
norm_eps = 1e-06

MESH = pl.DeviceIdType.MESH
F32 = jnp.float32
BF16 = jnp.bfloat16


def position_tables(col_pairs, row_couples, model_width):
    quarter = model_width // 4
    frequency = np.exp(-math.log(10000.0) * np.arange(quarter) / quarter)

    def part(count):
        angle = np.arange(count)[:, None] * frequency[None, :]
        return np.concatenate([np.sin(angle), np.cos(angle)], axis=1)

    row_pos = np.zeros((row_couples, model_width), np.float32)
    row_pos[:, : model_width // 2] = part(row_couples)
    col_pos = np.zeros((col_pairs, model_width), np.float32)
    col_pos[:, model_width // 2 :] = part(col_pairs)
    return row_pos, col_pos


def plan_tables():
    beta = 1e-4 + (0.02 - 1e-4) * np.arange(plan_length) / (plan_length - 1)
    now = np.exp(np.cumsum(np.log(1.0 - beta)))
    stride = plan_length // STEPS
    before = np.concatenate([np.ones(stride), now[:-stride]])
    keep = np.sqrt(before) / np.sqrt(now)
    step = np.sqrt(1.0 - before) - keep * np.sqrt(1.0 - now)
    return keep.astype(np.float32), step.astype(np.float32)


def nt(a, b):
    return lax.dot_general(a, b, (((1,), (1,)), ((), ())), preferred_element_type=F32)


def tn(a, b):
    return lax.dot_general(a, b, (((0,), (0,)), ((), ())), preferred_element_type=F32)


def nn(a, b):
    return jnp.dot(a, b, preferred_element_type=F32)


def exact(a, b):
    return jnp.dot(a, b, preferred_element_type=F32, precision=lax.Precision.HIGHEST)


def iota(shape, dim):
    return lax.broadcasted_iota(jnp.int32, shape, dim)


def kernel(
    n_win,
    off_ref,
    blend_ref,
    step_ref,
    keep_ref,
    stepc_ref,
    lat_hbm,
    text_hbm,
    mod_hbm,
    qkv_hbm,
    wout_hbm,
    pw_hbm,
    fw_hbm,
    rowpos_hbm,
    colpos_hbm,
    prev_ref,
    noise_ref,
    lat,
    text,
    mod,
    wqkv,
    wown,
    woth,
    pw,
    fw,
    rowpos,
    colpos,
    slabs,
    win32,
    emb,
    normed,
    proj,
    kall,
    vall,
    att_send,
    att_recv,
    att_own,
    mixed,
    blend_own,
    blend_send,
    blend_recv,
    local_sem,
    send_sem,
    recv_sem,
):
    c = lax.axis_index("cfg")
    w = lax.axis_index("win")
    right = lax.rem(w + 1, n_win)
    left = lax.rem(w + n_win - 1, n_win)
    first = c == 0

    names = (
        (lat_hbm, lat),
        (pw_hbm, pw),
        (rowpos_hbm, rowpos),
        (colpos_hbm, colpos),
        (mod_hbm, mod),
        (qkv_hbm, wqkv),
        (text_hbm, text),
        (wout_hbm, wown),
        (fw_hbm, fw),
    )
    loads = [
        pltpu.make_async_copy(src, dst, local_sem.at[i]) for i, (src, dst) in enumerate(names)
    ]
    barrier = pltpu.get_barrier_semaphore()
    for target in ((c, left), (c, right), (1 - c, w)):
        pl.semaphore_signal(barrier, inc=1, device_id=target, device_id_type=MESH)
    for load in loads:
        load.start()
    lat_load, pw_load, row_load, col_load, mod_load, qkv_load, text_load, own_load, fw_load = loads

    lat_load.wait()
    slab = jnp.transpose(lat[...])
    slabs[1] = slab.astype(BF16)

    pl.semaphore_wait(barrier, 3)

    def send(i, src, dst, target):
        copy = pltpu.make_async_remote_copy(
            src_ref=src,
            dst_ref=dst,
            send_sem=send_sem.at[i],
            recv_sem=recv_sem.at[i],
            device_id=target,
            device_id_type=MESH,
        )
        copy.start()
        return copy

    to_right = send(0, slabs.at[1], slabs.at[0], (c, right))
    to_left = send(1, slabs.at[1], slabs.at[2], (c, left))
    weights = send(2, wout_hbm, woth, (1 - c, w))

    half_rows = slab.shape[0] // 2
    own_rows = jnp.where(first, slab[:half_rows], slab[half_rows:])
    lane = iota((half_rows, 128), 1)
    picked = jnp.concatenate(
        [jnp.where(lane % 4 == ch, own_rows, 0.0) for ch in range(4)], axis=0
    )
    column_of = (iota((128, 128), 0) // 4 == iota((128, 128), 1)).astype(F32)
    lat_out = exact(picked, column_of)

    off = off_ref[0]
    moment = step_ref[0]

    src = iota((384, 256), 0)
    dst = iota((384, 256), 1)
    shift = (src == dst + 4 * (32 - off)).astype(F32).astype(BF16)

    pw_load.wait()
    feature = iota((256, 16), 0)
    wanted = (feature % 8) // 4 * 8 + feature % 4 * 2 + feature // 128
    embed_w = nn((iota((256, 16), 1) == wanted).astype(F32).astype(BF16), pw[...]).astype(BF16)

    row_load.wait()
    col_load.wait()
    mod_load.wait()
    modulate = mod[lax.div(moment * STEPS, plan_length)]
    mod_shift = modulate[0:1]
    mod_scale = 1.0 + modulate[1:2]
    gate = modulate[2:3]
    out_scale = 1.0 + modulate[3:4]

    text_load.wait()
    heads = 4
    for b in range(2):
        keys = text[b, 0].astype(F32)
        vals = text[b, 1].astype(F32)
        zeros_k = jnp.zeros((8, HEAD_DIM), F32)
        for h in range(heads):
            part = keys[h * HEAD_DIM : (h + 1) * HEAD_DIM]
            kt = jnp.transpose(part)
            kall[h, 512 + 128 * b : 640 + 128 * b, :] = jnp.concatenate(
                [kt, zeros_k], axis=0
            ).astype(BF16)
            vt = jnp.concatenate(
                [vals[h * HEAD_DIM : (h + 1) * HEAD_DIM], jnp.ones((8, 120), F32)], axis=0
            )
            vall[h, :, 512 + 128 * b : 632 + 128 * b] = vt.astype(BF16)
            vall[h, :, 632 + 128 * b : 640 + 128 * b] = jnp.zeros((80, 8), BF16)

    to_right.wait_recv()
    to_left.wait_recv()
    all_slabs = jnp.concatenate([slabs[0], slabs[1], slabs[2]], axis=1)
    window = nn(all_slabs, shift)
    win32[0] = window[:, :128]
    win32[1] = window[:, 128:]

    token_mask = iota((128, 128), 0) // 8 == iota((128, 128), 1) // 8
    for half in range(2):
        groups = []
        for g in range(2):
            both = []
            for dh in range(2):
                low = win32[g, pl.ds(dh, 8, stride=2), :]
                high = win32[g, pl.ds(16 + dh, 8, stride=2), :]
                piece = jnp.where(first, high, low) if half == 0 else jnp.where(first, low, high)
                both.append(
                    jnp.where(token_mask, jnp.concatenate([piece] * 16, axis=0), 0.0)
                )
            groups.append(jnp.concatenate(both, axis=1))
        lhs = jnp.concatenate(groups, axis=0).astype(BF16)
        emb[half * 256 : (half + 1) * 256, :] = nn(lhs, embed_w)

    rp = rowpos[...]
    rp_half = (jnp.where(first, rp[8:], rp[:8]), jnp.where(first, rp[:8], rp[8:]))
    model_width = emb.shape[1]

    def center(values):
        centered = values - jnp.mean(values, axis=-1, keepdims=True)
        variance = jnp.mean(centered * centered, axis=-1, keepdims=True)
        return centered * lax.rsqrt(variance + norm_eps)

    for half in range(2):
        for chunk in range(8):
            at = half * 256 + chunk * 32
            values = emb[at : at + 32, :].reshape(4, 8, model_width)
            values = values + rp_half[half][None]
            values = values + colpos[chunk * 4 : chunk * 4 + 4, :].reshape(4, 1, model_width)
            values = values.reshape(32, model_width)
            if half == 1:
                emb[at : at + 32, :] = values
            normed[at : at + 32, :] = (center(values) * mod_scale + mod_shift).astype(BF16)

    qkv_load.wait()
    proj[...] = nt(wqkv[...], normed[...])

    for h in range(heads):
        kt = proj[288 + h * HEAD_DIM : 288 + (h + 1) * HEAD_DIM, :]
        kall[h, 0:512, :] = jnp.transpose(kt).astype(BF16)
        vt = proj[576 + h * HEAD_DIM : 576 + (h + 1) * HEAD_DIM, :]
        vall[h, :, 0:512] = jnp.concatenate([vt, jnp.ones((8, 512), F32)], axis=0).astype(BF16)

    factor = math.log2(math.e) / math.sqrt(HEAD_DIM)

    def attend(h, half):
        q = (
            proj[h * HEAD_DIM : (h + 1) * HEAD_DIM, half * 256 : (half + 1) * 256] * factor
        ).astype(BF16)
        scores = nn(kall[h], q)
        own = scores[:512]
        own_max = jnp.max(own, axis=0, keepdims=True)
        own_exp = jnp.exp2(own - own_max).astype(BF16)
        own_out = nn(vall[h, :, 0:512], own_exp)
        result = []
        for b in range(2):
            cap = scores[512 + 128 * b : 632 + 128 * b]
            cap_max = jnp.max(cap, axis=0, keepdims=True)
            cap_exp = jnp.concatenate(
                [jnp.exp2(cap - cap_max), jnp.zeros((8, 256), F32)], axis=0
            ).astype(BF16)
            cap_out = nn(vall[h, :, 512 + 128 * b : 640 + 128 * b], cap_exp)
            top = jnp.maximum(own_max, cap_max)
            w_own = jnp.exp2(own_max - top)
            w_cap = jnp.exp2(cap_max - top)
            total = w_own * own_out[72:73] + w_cap * cap_out[72:73]
            w_own = w_own / total
            w_cap = w_cap / total
            result.append(own_out[:72] * w_own + cap_out[:72] * w_cap)
        return result

    att_copies = []
    for half in range(2):
        for pair in range(2):
            one = attend(2 * pair, half)
            two = attend(2 * pair + 1, half)
            for b in range(2):
                both = jnp.concatenate([one[b], two[b]], axis=0).astype(BF16)
                if half == 0:
                    att_send[pair, :, b * 256 : (b + 1) * 256] = both
                else:
                    att_own[pair * 144 : (pair + 1) * 144, b * 256 : (b + 1) * 256] = both
            if half == 0:
                att_copies.append(
                    send(3 + pair, att_send.at[pair], att_recv.at[pair], (1 - c, w))
                )

    own_load.wait()
    mixed[...] = tn(att_own[...], wown[...])
    weights.wait_recv()
    for copy in att_copies:
        copy.wait_recv()
    other = jnp.concatenate([att_recv[0], att_recv[1]], axis=0)
    mixed[...] += tn(other, woth[...])

    fw_load.wait()
    eps = []
    for b in range(2):
        for chunk in range(8):
            at = chunk * 32
            values = emb[256 + at : 288 + at, :] + gate * mixed[b * 256 + at : b * 256 + at + 32, :]
            normed[b * 256 + at : b * 256 + at + 32, :] = (center(values) * out_scale).astype(BF16)
    for b in range(2):
        eps.append(nt(normed[b * 256 : (b + 1) * 256, :], fw[...]))
    blend = blend_ref[0].astype(F32)
    guided = (eps[1] + guidance_scale * (eps[0] - eps[1])) * blend
    guided_t = jnp.transpose(guided)

    start = 16 - off
    row = iota((16, 256), 0)
    keep = (iota((16, 256), 1) % 8) == (row // 2)
    spread = None
    for dw in range(2):
        blocks = []
        for ch in range(4):
            f = dw * 8 + ch * 2
            even = jnp.broadcast_to(guided_t[f : f + 1], (16, 256))
            odd = jnp.broadcast_to(guided_t[f + 1 : f + 2], (16, 256))
            blocks.append(jnp.where(keep, jnp.where(row % 2 == 0, even, odd), 0.0))
        place = (iota((256, 128), 1) == (iota((256, 128), 0) // 8) * 2 + dw + start).astype(F32)
        term = exact(jnp.concatenate(blocks, axis=0), place)
        spread = term if spread is None else spread + term
    lanes = iota((8, 128), 1)
    cover = jnp.where((lanes >= start) & (lanes < start + 64), blend, 0.0)
    laid = jnp.concatenate([spread, cover], axis=0)
    blend_send[0] = pltpu.roll(laid, 128 - 48, axis=1)
    blend_send[1] = pltpu.roll(laid, 16, axis=1)
    blend_right = send(5, blend_send.at[0], blend_recv.at[0], (c, right))
    blend_left = send(6, blend_send.at[1], blend_recv.at[1], (c, left))
    kept = pltpu.roll(laid, 128 - 16, axis=1)
    blend_right.wait_recv()
    blend_left.wait_recv()
    from_left = blend_recv[0]
    from_right = blend_recv[1]
    lanes72 = iota((72, 128), 1)
    total = (
        kept
        + jnp.where(lanes72 < 32, from_left, 0.0)
        + jnp.where((lanes72 >= 16) & (lanes72 < 32), from_right, 0.0)
    )
    noise = total[:64] / total[64:65]
    noise_ref[...] = noise[:, :32]
    prev_ref[...] = (keep_ref[moment] * lat_out + stepc_ref[moment] * noise)[:, :32]

    for copy in [to_right, to_left, weights, blend_right, blend_left] + att_copies:
        copy.wait_send()


def on_device(
    n_win,
    latent,
    text_kv,
    modulation,
    qkv_weight,
    out_weight,
    patch_weight,
    final_weight,
    offsets,
    blend_weights,
    step_index,
):
    slab_cols, channels, row_count = latent.shape
    model_width = patch_weight.shape[1]
    half_attn = out_weight.shape[0]
    row_pos, col_pos = position_tables(slab_cols, row_count // 2, model_width)
    keep, step = plan_tables()
    lat = latent.reshape(slab_cols * channels, row_count)
    text = text_kv.transpose(0, 1, 3, 2)
    qkv = qkv_weight.transpose(1, 2, 0).reshape(3 * half_attn, model_width)
    fw = final_weight.T
    hbm = pl.BlockSpec(memory_space=pltpu.HBM)
    smem = pl.BlockSpec(memory_space=pltpu.SMEM)
    vmem = pl.BlockSpec(memory_space=pltpu.VMEM)
    half_rows = row_count // 2
    out = jax.ShapeDtypeStruct((channels * half_rows, slab_cols), F32)
    prev, noise = pl.pallas_call(
        functools.partial(kernel, n_win),
        out_shape=(out, out),
        in_specs=[smem] * 5 + [hbm] * 9,
        out_specs=(vmem, vmem),
        scratch_shapes=[
            pltpu.VMEM(lat.shape, F32),
            pltpu.VMEM(text.shape, BF16),
            pltpu.VMEM(modulation.shape, F32),
            pltpu.VMEM(qkv.shape, BF16),
            pltpu.VMEM(out_weight.shape, BF16),
            pltpu.VMEM(out_weight.shape, BF16),
            pltpu.VMEM(patch_weight.shape, BF16),
            pltpu.VMEM(fw.shape, BF16),
            pltpu.VMEM(row_pos.shape, F32),
            pltpu.VMEM(col_pos.shape, F32),
            pltpu.VMEM((3, 32, 128), BF16),
            pltpu.VMEM((2, 32, 128), F32),
            pltpu.VMEM((512, model_width), F32),
            pltpu.VMEM((512, model_width), BF16),
            pltpu.VMEM((3 * half_attn, 512), F32),
            pltpu.VMEM((4, 768, HEAD_DIM), BF16),
            pltpu.VMEM((4, 80, 768), BF16),
            pltpu.VMEM((2, 144, 512), BF16),
            pltpu.VMEM((2, 144, 512), BF16),
            pltpu.VMEM((288, 512), BF16),
            pltpu.VMEM((512, model_width), F32),
            pltpu.VMEM((72, 128), F32),
            pltpu.VMEM((2, 72, 128), F32),
            pltpu.VMEM((2, 72, 128), F32),
            pltpu.SemaphoreType.DMA((9,)),
            pltpu.SemaphoreType.DMA((7,)),
            pltpu.SemaphoreType.DMA((7,)),
        ],
        compiler_params=pltpu.CompilerParams(
            collective_id=0, has_side_effects=True, vmem_limit_bytes=56 * 1024 * 1024
        ),
    )(
        offsets,
        blend_weights,
        step_index,
        jnp.asarray(keep),
        jnp.asarray(step),
        lat,
        text,
        modulation,
        qkv,
        out_weight,
        patch_weight,
        fw,
        jnp.asarray(row_pos),
        jnp.asarray(col_pos),
    )

    def placed(array):
        return array.reshape(channels, half_rows, slab_cols).transpose(2, 0, 1)

    return placed(prev), placed(noise)


def solution(mesh):
    in_specs = (
        P("win", None, None),
        P(None, None, None, "cfg"),
        P(),
        P(None, None, "cfg"),
        P("cfg", None),
        P(),
        P(),
        P("win"),
        P("win"),
        P(),
    )
    out_specs = (P("win", None, "cfg"), P("win", None, "cfg"))
    return jax.shard_map(
        functools.partial(on_device, mesh.shape["win"]),
        mesh=mesh,
        in_specs=in_specs,
        out_specs=out_specs,
        check_vma=False,
    )
```

time: 131 us -> 48.1 us (0.37)
  starting transfers between devices: 46.6 us -> 0 us
  Pallas kernels: 0 us -> 42.5 us
  matrix products: 30 us -> 0 us
  local copies, waits for them, and re-layouts: 22.8 us -> 2.75 us
  other arithmetic: 16.4 us -> 0 us
  waiting for transfers between devices: 8.44 us -> 0 us
  between operations: 5.15 us -> 2.58 us
    pallas_call x0 -> x1, Pallas kernels: none -> 42.5 us  [on_device(): pl.pallas_call(functools.partial(kernel, n_win), out_shape=(out, out), in...]
    ppermute x7 -> x0, starting transfers between devices: 41 us -> none  [the longest x6 35.9 us: from_behind(): lax.ppermute(array, axis, [(i, (i + by) % size) for i in range(size)])]
    dot_general x20 -> x0, matrix products: 30 us -> none  [the longest x4 7.94 us: one_head(): jnp.einsum('roz,zt->rot', self_softmax_weights, value_tile, preferred_ele...]
    reduce_sum x14 -> x0, other arithmetic: 12.5 us -> none  [the longest x8 8.02 us: one_head(): totals = jnp.sum(own_exp, axis=-1) + jnp.sum(text_exp, axis=-1)]
    all_to_all x1 -> x0, waiting for transfers between devices: 6.16 us -> none  [summed_on_arrival(): lax.all_to_all(tiles, axis, split_axis=0, concat_axis=0, tiled=True)]
    all_to_all x1 -> x0, starting transfers between devices: 5.55 us -> none  [summed_on_arrival(): lax.all_to_all(tiles, axis, split_axis=0, concat_axis=0, tiled=True)]
    mul x4 -> x0, local copies, waits for them, and re-layouts: 5.23 us -> none  [one_head(): jnp.einsum('qd,kd->qk', query_tile, key_block, preferred_element_type=jnp...]
    while x16 -> x0, local copies, waits for them, and re-layouts: 3.32 us -> none
  transfers between devices with their start and end apart: 8 -> 0, of which waited for: 3 -> 0; matrix products, arithmetic and copies ran while one was open for 12% -> 0% of each run, Pallas kernels for 0% -> 0%
where the time goes in v1:
time: 48.1 us; the launch traced here: 47.8 us
  Pallas kernels  42.5 us (88%)
  local copies, waits for them, and re-layouts  2.75 us (6%)
  between operations  2.58 us (5%)
    pallas_call x1, Pallas kernels, on_device(): pl.pallas_call(functools.partial(kernel, n_win), out_shape=(out, out), in...  42.5 us
    unnamed x2, local copies, waits for them, and re-layouts  2.75 us

profile of v1, /device:TPU:16, one launch (start us, length us, event | category | flops | bytes accessed | tf_op | source)
XLA Modules:
  0.0 47.8 jit_solution(7835067168853511091)
XLA Ops:
  2.6 42.5 %shard_map.149 = (f32[64,32]{1,0:T(8,128)}, f32[64,32]{1,0:T(8,128)}) custom-call(s32[1]{0:T(128)S(6)} %copy.18.off_ref, s32[1]{0:T(128)S(6)} %copy.19.blend_ref, s32[1]{0:T(128)S(6)} %copy.20.step_ref, f32[1000]{0:T(1024)} %constant.8.clone.keep_ref, f32[1000]{0:T(1024)} %constant.9.clone.stepc_ref, f32[128,32]{1,0:T(8,128)} %bitcast.14, ...), custom_call_target="tpu_custom_call" | custom-call | tf_op jit(solution)/shard_map/pallas_call | solution.py:396
  45.1 1.4 %copy.21 = f32[32,4,16]{0,2,1:T(8,128)} copy(f32[32,4,16]{0,2,1:T(8,128)} %bitcast.17) | data formatting | bytes 16384
  46.4 1.4 %copy.22 = f32[32,4,16]{0,2,1:T(8,128)} copy(f32[32,4,16]{0,2,1:T(8,128)} %bitcast.16) | data formatting | bytes 16384
